TPU v7x, 256 devices: a whole 4x4x8 slice. The times are simulated.
256 devices in a mesh: dp: 8 (over x, core), param: 32 (over y, z).
Axes of the slice: x: 4, y: 4, z: 8, core: 2. Of those that a mesh axis runs over, the one named last changes fastest.
Arguments:
- train_grads: bfloat16 [7168, 212992], P('dp', 'param'), as said below
- query_grads: bfloat16 [256, 212992], P('dp', 'param'), as said below
Outputs:
- scores: float32 [256, 7168], P('param', 'dp')
Inputs may be any that keep to these rules, and one draw needn't show every extreme that they name: `train_grads`: finite real values. `query_grads`: finite real values.
All inputs are finite; a program needn't handle non-finite values.
Results may differ from a plain program's by a relative error of at most 0.0003.
Values may be sent and summed in bfloat16 or wider, within the bound.
A program may use at most 64 MiB of HBM per device.

v0:
```python
import jax
import jax.numpy as jnp
from jax import lax
from jax.sharding import PartitionSpec as P

epsilon = 1e-06


def in_blocks(x, dim, devices):
    lengths = x.shape
    pieces = x.reshape(*lengths[:dim], devices, lengths[dim] // devices, *lengths[dim + 1 :])
    return jnp.moveaxis(pieces, dim, 0)


def summed_on_arrival(x, axis, dim):
    devices = lax.axis_size(axis)
    pieces = lax.all_to_all(in_blocks(x, dim, devices), axis, 0, 0, tiled=True)
    return jnp.sum(pieces, axis=0)


def side_by_side(arrays, axis, dim, along):
    columns = [a.reshape(*a.shape[:along], -1) for a in arrays]
    both = jnp.concatenate(columns, axis=along)
    out, at, done = (summed_on_arrival(both, axis, dim), 0, [])
    for a, column in zip(arrays, columns):
        slab = out[..., at : at + column.shape[along]]
        done.append(slab.reshape(*slab.shape[:along], *a.shape[along:]))
        at += column.shape[along]
    return tuple(done)


def copy_for_each(x, axis):
    devices = lax.axis_size(axis)
    return lax.all_to_all(jnp.broadcast_to(x[None], (devices, *x.shape)), axis, 0, 0, tiled=True)


def taken_together(x, axis):
    everything = copy_for_each(x, axis)
    return jnp.sum(everything, axis=0)


def per_device(train_grads, query_grads):
    queries = lax.all_gather(query_grads, "dp", axis=0, tiled=True)
    products = lax.dot_general(
        queries, train_grads, (((1,), (1,)), ((), ())), preferred_element_type=jnp.float32
    )
    query_norm = jnp.sum(jnp.square(queries.astype(jnp.float32)), axis=1)
    train_norm = jnp.sum(jnp.square(train_grads.astype(jnp.float32)), axis=1)
    products, query_norm = side_by_side((products, query_norm), "param", 0, 1)
    train_norm = taken_together(train_norm, "param")
    return (
        products
        * lax.rsqrt(query_norm + epsilon)[:, None]
        * lax.rsqrt(train_norm + epsilon)[None, :]
    )


def solution(mesh):
    return jax.shard_map(
        per_device,
        mesh=mesh,
        in_specs=(P("dp", "param"), P("dp", "param")),
        out_specs=P("param", "dp"),
        check_vma=False,
    )
```

profile of v0, /device:TPU:32, one launch (start us, length us, event | category | flops | bytes accessed | tf_op | source)
XLA Modules:
  0.0 102.4 jit_solution(12826004121880036399)
XLA Ops:
  6.5 0.0 all-gather.2.cloned.1.call-start
  6.5 0.7 all-gather.2.cloned.1.call-update
  7.3 6.8 %multiply_reduce_fusion = f32[896]{0:T(1024)S(1)} fusion(bf16[896,6656]{1,0:T(8,128)(2,1)} %param.2), kind=kLoop, calls=%fused_computation | loop fusion | flops 17890432 | bytes 11931136 | tf_op jit(solution)/shard_map/reduce_sum | solution.py:48
  14.0 0.7 broadcast_in_dim.2
  14.7 11.4 %all-to-all-start.1 = ((f32[32,1,896]{2,1,0:T(1,128)}), f32[32,1,896]{2,1,0:T(1,128)S(1)}, u32[]{:S(2)}, u32[]{:S(2)}) async-start(f32[32,1,896]{2,1,0:T(1,128)} %broadcast_in_dim.2), calls=%async_computation.1 | async-start | bytes 229376 | tf_op jit(solution)/shard_map/all_to_all | solution.py:34
  26.1 17.0 %all-gather.2.cloned.1.call-done = bf16[256,6656]{1,0:T(8,128)(2,1)} async-done(((bf16[32,6656]{1,0:T(8,128)(2,1)}), bf16[256,6656]{1,0:T(8,128)(2,1)}) %all-gather.2.cloned.1.call-update) | async-done | bytes 3407888 | tf_op jit(solution)/shard_map/all_gather | solution.py:43
  43.1 0.0 copy-start
  43.1 10.6 %convolution_bitcast_fusion = f32[32,8,896]{2,1,0:T(8,128)S(1)} fusion(bf16[256,6656]{1,0:T(8,128)(2,1)} %all-gather.2.cloned.1.call-done, bf16[896,6656]{1,0:T(8,128)(2,1)} %param.2), kind=kOutput, calls=%fused_computation.2 | convolution fusion | flops 3053453312 | bytes 16252928 | tf_op jit(solution)/shard_map/dot_general | solution.py:44
  53.8 0.0 copy-done
  53.8 0.8 multiply_reduce_fusion.1
  54.5 0.2 concatenate.11
  54.7 1.1 %pad_maximum_fusion = f32[32,8,897]{2,1,0:T(8,128)} fusion(f32[32,8,1]{2,1,0:T(8,128)S(1)} %concatenate.11, f32[32,8,896]{2,1,0:T(8,128)S(1)} %convolution_bitcast_fusion), kind=kLoop, calls=%fused_computation.3 | loop fusion | flops 229632 | bytes 1837056 | tf_op jit(solution)/shard_map/concatenate | solution.py:23
  55.8 0.0 all-to-all-done.1
  55.9 10.1 %all-to-all-start = ((f32[32,8,897]{2,1,0:T(8,128)}), f32[32,8,897]{2,1,0:T(8,128)S(1)}, u32[]{:S(2)}, u32[]{:S(2)}) async-start(f32[32,8,897]{2,1,0:T(8,128)} %pad_maximum_fusion), calls=%async_computation | async-start | bytes 2097152 | tf_op jit(solution)/shard_map/all_to_all | solution.py:17
  65.9 0.1 reduce_sum.39
  66.0 28.6 %all-to-all-done = f32[32,8,897]{2,1,0:T(8,128)S(1)} async-done(((f32[32,8,897]{2,1,0:T(8,128)}), f32[32,8,897]{2,1,0:T(8,128)S(1)}, u32[]{:S(2)}, u32[]{:S(2)}) %all-to-all-start) | async-done | bytes 918560 | tf_op jit(solution)/shard_map/all_to_all | solution.py:17
  94.7 0.1 reduce_sum.37
  94.7 0.1 fusion.2
  94.9 0.7 fusion
  (1 shorter events, 0.0 us)
Async XLA Ops:
  6.5 36.6 %all-gather.2.cloned.1.call-start = ((), (), s32[]{:S(2)}) async-start(), calls=%async_computation.2 | async-start | bytes 3833856 | tf_op jit(solution)/shard_map/all_gather | solution.py:43
  14.7 41.1 %all-to-all-start.1 = ((f32[32,1,896]{2,1,0:T(1,128)}), f32[32,1,896]{2,1,0:T(1,128)S(1)}, u32[]{:S(2)}, u32[]{:S(2)}) async-start(f32[32,1,896]{2,1,0:T(1,128)} %broadcast_in_dim.2), calls=%async_computation.1 | async-start | bytes 229376 | tf_op jit(solution)/shard_map/all_to_all | solution.py:34
  43.1 10.7 %copy-start = (bf16[256,6656]{1,0:T(8,128)(2,1)S(1)}, bf16[256,6656]{1,0:T(8,128)(2,1)}, u32[]{:S(2)}) copy-start(bf16[256,6656]{1,0:T(8,128)(2,1)} %all-gather.2.cloned.1.call-done) | copy-start | bytes 10223620
  55.9 38.8 %all-to-all-start = ((f32[32,8,897]{2,1,0:T(8,128)}), f32[32,8,897]{2,1,0:T(8,128)S(1)}, u32[]{:S(2)}, u32[]{:S(2)}) async-start(f32[32,8,897]{2,1,0:T(8,128)} %pad_maximum_fusion), calls=%async_computation | async-start | bytes 2097152 | tf_op jit(solution)/shard_map/all_to_all | solution.py:17
Sparse Core Ops, SparseCore 0:
  9.2 33.8 all-gather.1
where the time goes:
time: 103 us; the launch traced here: 102 us
  waiting for transfers between devices  46.3 us (45%)
  starting transfers between devices  21.4 us (21%)
  between operations  13.4 us (13%)
  matrix products  10.6 us (10%)
  other arithmetic  9.61 us (9%)
    all_to_all x1, waiting for transfers between devices, summed_on_arrival(): pieces = lax.all_to_all(in_blocks(x, dim, devices), axis, 0, 0, tiled=True)  28.6 us
    all_gather x1, waiting for transfers between devices, per_device(): queries = lax.all_gather(query_grads, 'dp', axis=0, tiled=True)  17 us
    all_to_all x1, starting transfers between devices, copy_for_each(): lax.all_to_all(jnp.broadcast_to(x[None], (devices, *x.shape)), axis, 0, 0...  11.4 us
    dot_general x1, matrix products, per_device(): lax.dot_general(queries, train_grads, (((1,), (1,)), ((), ())), preferred...  10.6 us
    all_to_all x1, starting transfers between devices, summed_on_arrival(): pieces = lax.all_to_all(in_blocks(x, dim, devices), axis, 0, 0, tiled=True)  10.1 us
    reduce_sum x1, other arithmetic, per_device(): train_norm = jnp.sum(jnp.square(train_grads.astype(jnp.float32)), axis=1)  6.77 us
  transfers between devices with their start and end apart: 3, of which 2 were waited for; matrix products, arithmetic and copies ran while one was open for 20% of the time, Pallas kernels for 0%

commit v1 on v0

--- a/solution.py
+++ b/solution.py
@@ -40,7 +40,16 @@
 
 
 def per_device(train_grads, query_grads):
-    queries = lax.all_gather(query_grads, "dp", axis=0, tiled=True)
+    ways = lax.axis_size("dp")
+    up = [(d, (d + 1) % ways) for d in range(ways)]
+    down = [(d, (d - 1) % ways) for d in range(ways)]
+    earlier, later = ([query_grads], [query_grads])
+    for _ in range(ways // 2):
+        earlier.append(lax.ppermute(earlier[-1], "dp", up))
+    for _ in range((ways - 1) // 2):
+        later.append(lax.ppermute(later[-1], "dp", down))
+    line = jnp.concatenate([*earlier[::-1], *later[1:]], axis=0)
+    queries = jnp.roll(line, (lax.axis_index("dp") - ways // 2) * query_grads.shape[0], axis=0)
     products = lax.dot_general(
         queries, train_grads, (((1,), (1,)), ((), ())), preferred_element_type=jnp.float32
     )

time: 103 us -> 122 us (1.18)
  local copies, waits for them, and re-layouts: 0.93 us -> 25.2 us
  between operations: 13.4 us -> 0.09 us
  starting transfers between devices: 21.4 us -> 29.5 us
  matrix products: 10.6 us -> 6.6 us
  other arithmetic: 9.61 us -> 12.7 us
    unnamed x2 -> x21, local copies, waits for them, and re-layouts: 0.01 us -> 23.5 us
    ppermute x0 -> x7, waiting for transfers between devices: none -> 20.7 us  [the longest x4 20.7 us: per_device(): earlier.append(lax.ppermute(earlier[-1], 'dp', up))]
    all_gather x1 -> x0, waiting for transfers between devices: 17 us -> none  [per_device(): queries = lax.all_gather(query_grads, 'dp', axis=0, tiled=True)]
    ppermute x0 -> x7, starting transfers between devices: none -> 8.32 us  [the longest x3 8.31 us: per_device(): later.append(lax.ppermute(later[-1], 'dp', down))]
    dot_general x1, matrix products: 10.6 us -> 6.6 us  [per_device(): lax.dot_general(queries, train_grads, (((1,), (1,)), ((), ())), preferred...]
    all_to_all x1, waiting for transfers between devices: 28.6 us -> 26.3 us  [summed_on_arrival(): pieces = lax.all_to_all(in_blocks(x, dim, devices), axis, 0, 0, tiled=True)]
    reduce_sum x1, other arithmetic: 0.76 us -> 2.72 us  [per_device(): query_norm = jnp.sum(jnp.square(queries.astype(jnp.float32)), axis=1)]
  transfers between devices with their start and end apart: 3 -> 9, of which waited for: 2 -> 4; matrix products, arithmetic and copies ran while one was open for 20% -> 35% of each run, Pallas kernels for 0% -> 0%
where the time goes in v1:
time: 122 us; the launch traced here: 121 us
  waiting for transfers between devices  47 us (39%)
  starting transfers between devices  29.5 us (24%)
  local copies, waits for them, and re-layouts  25.2 us (21%)
  other arithmetic  12.7 us (10%)
  matrix products  6.6 us (5%)
    all_to_all x1, waiting for transfers between devices, summed_on_arrival(): pieces = lax.all_to_all(in_blocks(x, dim, devices), axis, 0, 0, tiled=True)  26.3 us
    unnamed x21, local copies, waits for them, and re-layouts  23.5 us
    ppermute x4, waiting for transfers between devices, per_device(): earlier.append(lax.ppermute(earlier[-1], 'dp', up))  20.7 us
    all_to_all x1, starting transfers between devices, copy_for_each(): lax.all_to_all(jnp.broadcast_to(x[None], (devices, *x.shape)), axis, 0, 0...  11.4 us
    all_to_all x1, starting transfers between devices, summed_on_arrival(): pieces = lax.all_to_all(in_blocks(x, dim, devices), axis, 0, 0, tiled=True)  9.78 us
    ppermute x3, starting transfers between devices, per_device(): later.append(lax.ppermute(later[-1], 'dp', down))  8.31 us
    reduce_sum x1, other arithmetic, per_device(): train_norm = jnp.sum(jnp.square(train_grads.astype(jnp.float32)), axis=1)  6.77 us
    dot_general x1, matrix products, per_device(): lax.dot_general(queries, train_grads, (((1,), (1,)), ((), ())), preferred...  6.6 us
  transfers between devices with their start and end apart: 9, of which 4 were waited for; matrix products, arithmetic and copies ran while one was open for 35% of the time, Pallas kernels for 0%

profile of v1, /device:TPU:32, one launch (start us, length us, event | category | flops | bytes accessed | tf_op | source)
XLA Modules:
  0.0 121.1 jit_solution(9864693750480523951)
XLA Ops:
  0.0 9.0 %collective-permute-done = bf16[32,6656]{1,0:T(8,128)(2,1)S(1)} collective-permute-done((bf16[32,6656]{1,0:T(8,128)(2,1)}, bf16[32,6656]{1,0:T(8,128)(2,1)S(1)}, u32[]{:S(2)}, u32[]{:S(2)}) %collective-permute-start) | collective-permute-done | bytes 426016 | tf_op jit(solution)/shard_map/ppermute | solution.py:48
  9.0 3.0 %collective-permute-start.4 = (bf16[32,6656]{1,0:T(8,128)(2,1)}, bf16[32,6656]{1,0:T(8,128)(2,1)}, u32[]{:S(2)}, u32[]{:S(2)}) collective-permute-start(bf16[32,6656]{1,0:T(8,128)(2,1)} %param.3), channel_id=1, source_target_pairs={{0,224},{32,0},{64,32},{96,64},{128,96},{160,128},{192,160},{224,1... | collective-permute-start | bytes 1277960 | tf_op jit(solution)/shard_map/ppermute | solution.py:50
  11.9 5.8 %collective-permute-done.1 = bf16[32,6656]{1,0:T(8,128)(2,1)S(1)} collective-permute-done((bf16[32,6656]{1,0:T(8,128)(2,1)S(1)}, bf16[32,6656]{1,0:T(8,128)(2,1)S(1)}, u32[]{:S(2)}, u32[]{:S(2)}) %collective-permute-start.1) | collective-permute-done | bytes 426016 | tf_op jit(solution)/shard_map/ppermute | solution.py:48
  18.5 3.0 %collective-permute-start.5 = (bf16[32,6656]{1,0:T(8,128)(2,1)}, bf16[32,6656]{1,0:T(8,128)(2,1)}, u32[]{:S(2)}, u32[]{:S(2)}) collective-permute-start(bf16[32,6656]{1,0:T(8,128)(2,1)} %collective-permute-done.4), channel_id=1, source_target_pairs={{0,224},{32,0},{64,32},{96,64},{128,96},{160,128},{192,160},{224,1... | collective-permute-start | bytes 1277960 | tf_op jit(solution)/shard_map/ppermute | solution.py:50
  21.5 5.9 %collective-permute-done.2 = bf16[32,6656]{1,0:T(8,128)(2,1)} collective-permute-done((bf16[32,6656]{1,0:T(8,128)(2,1)S(1)}, bf16[32,6656]{1,0:T(8,128)(2,1)}, u32[]{:S(2)}, u32[]{:S(2)}) %collective-permute-start.2) | collective-permute-done | bytes 426016 | tf_op jit(solution)/shard_map/ppermute | solution.py:48
  27.4 6.8 %multiply_reduce_fusion = f32[896]{0:T(1024)S(1)} fusion(bf16[896,6656]{1,0:T(8,128)(2,1)} %param.2), kind=kLoop, calls=%fused_computation | loop fusion | flops 17890432 | bytes 11931136 | tf_op jit(solution)/shard_map/reduce_sum | solution.py:57
  34.9 11.4 %all-to-all-start.1 = ((f32[32,1,896]{2,1,0:T(1,128)}), f32[32,1,896]{2,1,0:T(1,128)S(1)}, u32[]{:S(2)}, u32[]{:S(2)}) async-start(f32[32,1,896]{2,1,0:T(1,128)} %broadcast_in_dim.2), calls=%async_computation.1 | async-start | bytes 229376 | tf_op jit(solution)/shard_map/all_to_all | solution.py:34
  46.3 2.4 %collective-permute-start.6 = (bf16[32,6656]{1,0:T(8,128)(2,1)}, bf16[32,6656]{1,0:T(8,128)(2,1)S(1)}, u32[]{:S(2)}, u32[]{:S(2)}) collective-permute-start(bf16[32,6656]{1,0:T(8,128)(2,1)} %collective-permute-done.5), channel_id=1, source_target_pairs={{0,224},{32,0},{64,32},{96,64},{128,96},{160,128},{192,160},{224,1... | collective-permute-start | bytes 1277960 | tf_op jit(solution)/shard_map/ppermute | solution.py:50
  48.7 2.5 %constant_dynamic-update-slice_fusion.15 = bf16[512,6656]{1,0:T(8,128)(2,1)} fusion(bf16[32,6656]{1,0:T(8,128)(2,1)} %collective-permute-done.3), kind=kLoop, calls=%fused_computation.21 | loop fusion | bytes 851968
  51.2 1.8 %constant_dynamic-update-slice_fusion.14 = bf16[512,6656]{1,0:T(8,128)(2,1)} fusion(bf16[512,6656]{1,0:T(8,128)(2,1)} %constant_dynamic-update-slice_fusion.15, bf16[32,6656]{1,0:T(8,128)(2,1)} %collective-permute-done.2), kind=kLoop, calls=%fused_computation.20 | loop fusion | bytes 851968
  53.0 1.8 %constant_dynamic-update-slice_fusion.13 = bf16[512,6656]{1,0:T(8,128)(2,1)} fusion(bf16[512,6656]{1,0:T(8,128)(2,1)} %constant_dynamic-update-slice_fusion.14, bf16[32,6656]{1,0:T(8,128)(2,1)} %copy-done.2), kind=kLoop, calls=%fused_computation.19 | loop fusion | bytes 851968
  56.4 1.8 %constant_dynamic-update-slice_fusion.10 = bf16[512,6656]{1,0:T(8,128)(2,1)} fusion(bf16[512,6656]{1,0:T(8,128)(2,1)} %constant_dynamic-update-slice_fusion.11, bf16[32,6656]{1,0:T(8,128)(2,1)} %collective-permute-done.4), kind=kLoop, calls=%fused_computation.16 | loop fusion | bytes 851968
  58.2 1.8 %constant_dynamic-update-slice_fusion.9 = bf16[512,6656]{1,0:T(8,128)(2,1)} fusion(bf16[512,6656]{1,0:T(8,128)(2,1)} %constant_dynamic-update-slice_fusion.10, bf16[32,6656]{1,0:T(8,128)(2,1)} %collective-permute-done.5), kind=kLoop, calls=%fused_computation.15 | loop fusion | bytes 851968
  60.0 0.8 constant_dynamic-update-slice_fusion.8
  60.8 1.8 %constant_dynamic-update-slice_fusion.7 = bf16[512,6656]{1,0:T(8,128)(2,1)} fusion(bf16[512,6656]{1,0:T(8,128)(2,1)} %constant_dynamic-update-slice_fusion.8, bf16[32,6656]{1,0:T(8,128)(2,1)} %collective-permute-done.3), kind=kLoop, calls=%fused_computation.13 | loop fusion | bytes 851968
  62.6 1.8 %constant_dynamic-update-slice_fusion.6 = bf16[512,6656]{1,0:T(8,128)(2,1)} fusion(bf16[512,6656]{1,0:T(8,128)(2,1)} %constant_dynamic-update-slice_fusion.7, bf16[32,6656]{1,0:T(8,128)(2,1)} %collective-permute-done.2), kind=kLoop, calls=%fused_computation.12 | loop fusion | bytes 851968
  64.4 1.8 %constant_dynamic-update-slice_fusion.5 = bf16[512,6656]{1,0:T(8,128)(2,1)} fusion(bf16[512,6656]{1,0:T(8,128)(2,1)} %constant_dynamic-update-slice_fusion.6, bf16[32,6656]{1,0:T(8,128)(2,1)} %copy-done.2), kind=kLoop, calls=%fused_computation.11 | loop fusion | bytes 851968
  67.8 1.8 %constant_dynamic-update-slice_fusion.2 = bf16[512,6656]{1,0:T(8,128)(2,1)} fusion(bf16[512,6656]{1,0:T(8,128)(2,1)} %constant_dynamic-update-slice_fusion.3, bf16[32,6656]{1,0:T(8,128)(2,1)} %collective-permute-done.4), kind=kLoop, calls=%fused_computation.8 | loop fusion | bytes 851968
  69.6 1.8 %constant_dynamic-update-slice_fusion.1 = bf16[512,6656]{1,0:T(8,128)(2,1)} fusion(bf16[512,6656]{1,0:T(8,128)(2,1)} %constant_dynamic-update-slice_fusion.2, bf16[32,6656]{1,0:T(8,128)(2,1)} %collective-permute-done.5), kind=kLoop, calls=%fused_computation.7 | loop fusion | bytes 851968
  72.2 6.6 %fusion.2 = f32[32,8,896]{2,1,0:T(8,128)} fusion(bf16[896,6656]{1,0:T(8,128)(2,1)S(1)} %copy-done, bf16[512,6656]{1,0:T(8,128)(2,1)} %constant_dynamic-update-slice_fusion, s32[]{:T(128)S(6)} %select_n.14), kind=kOutput, calls=%fused_computation.4 | convolution fusion | flops 3053453312 | bytes 16252932 | tf_op jit(solution)/shard_map/dot_general | solution.py:53
  78.8 2.7 %multiply_reduce_fusion.1 = f32[256]{0:T(256)S(1)} fusion(bf16[512,6656]{1,0:T(8,128)(2,1)} %constant_dynamic-update-slice_fusion, s32[]{:T(128)S(6)} %select_n.14), kind=kLoop, calls=%fused_computation.1 | loop fusion | flops 5111552 | bytes 3408900 | tf_op jit(solution)/shard_map/reduce_sum | solution.py:56
  81.7 2.3 %pad_maximum_fusion = f32[32,8,897]{2,1,0:T(8,128)} fusion(f32[32,8,1]{2,1,0:T(8,128)S(1)} %concatenate.18, f32[32,8,896]{2,1,0:T(8,128)} %fusion.2), kind=kLoop, calls=%fused_computation.5 | loop fusion | flops 229632 | bytes 1837056 | tf_op jit(solution)/shard_map/concatenate | solution.py:23
  84.0 9.8 %all-to-all-start = ((f32[32,8,897]{2,1,0:T(8,128)}), f32[32,8,897]{2,1,0:T(8,128)S(1)}, u32[]{:S(2)}, u32[]{:S(2)}) async-start(f32[32,8,897]{2,1,0:T(8,128)} %pad_maximum_fusion), calls=%async_computation | async-start | bytes 2097152 | tf_op jit(solution)/shard_map/all_to_all | solution.py:17
  93.9 26.3 %all-to-all-done = f32[32,8,897]{2,1,0:T(8,128)S(1)} async-done(((f32[32,8,897]{2,1,0:T(8,128)}), f32[32,8,897]{2,1,0:T(8,128)S(1)}, u32[]{:S(2)}, u32[]{:S(2)}) %all-to-all-start) | async-done | bytes 918560 | tf_op jit(solution)/shard_map/all_to_all | solution.py:17
  (27 shorter events, 6.7 us)
Async XLA Ops:
  0.0 55.6 %copy-start.1 = (bf16[32,6656]{1,0:T(8,128)(2,1)S(1)}, bf16[32,6656]{1,0:T(8,128)(2,1)}, u32[]{:S(2)}) copy-start(bf16[32,6656]{1,0:T(8,128)(2,1)} %param.3) | copy-start | bytes 1277956
  0.0 9.0 %collective-permute-start = (bf16[32,6656]{1,0:T(8,128)(2,1)}, bf16[32,6656]{1,0:T(8,128)(2,1)S(1)}, u32[]{:S(2)}, u32[]{:S(2)}) collective-permute-start(bf16[32,6656]{1,0:T(8,128)(2,1)} %param.3), channel_id=1, source_target_pairs={{0,32},{32,64},{64,96},{96,128},{128,160},{160,192},{192,224},{224... | collective-permute-start | bytes 1277960 | tf_op jit(solution)/shard_map/ppermute | solution.py:48
  9.0 8.8 %collective-permute-start.1 = (bf16[32,6656]{1,0:T(8,128)(2,1)S(1)}, bf16[32,6656]{1,0:T(8,128)(2,1)S(1)}, u32[]{:S(2)}, u32[]{:S(2)}) collective-permute-start(bf16[32,6656]{1,0:T(8,128)(2,1)S(1)} %collective-permute-done), channel_id=1, source_target_pairs={{0,32},{32,64},{64,96},{96,128},{128,160},{160,192},{192,224},{224... | collective-permute-start | bytes 1277960 | tf_op jit(solution)/shard_map/ppermute | solution.py:48
  9.0 9.5 %collective-permute-start.4 = (bf16[32,6656]{1,0:T(8,128)(2,1)}, bf16[32,6656]{1,0:T(8,128)(2,1)}, u32[]{:S(2)}, u32[]{:S(2)}) collective-permute-start(bf16[32,6656]{1,0:T(8,128)(2,1)} %param.3), channel_id=1, source_target_pairs={{0,224},{32,0},{64,32},{96,64},{128,96},{160,128},{192,160},{224,1... | collective-permute-start | bytes 1277960 | tf_op jit(solution)/shard_map/ppermute | solution.py:50
  17.7 0.8 copy-start.2
  18.5 8.9 %collective-permute-start.2 = (bf16[32,6656]{1,0:T(8,128)(2,1)S(1)}, bf16[32,6656]{1,0:T(8,128)(2,1)}, u32[]{:S(2)}, u32[]{:S(2)}) collective-permute-start(bf16[32,6656]{1,0:T(8,128)(2,1)S(1)} %collective-permute-done.1), channel_id=1, source_target_pairs={{0,32},{32,64},{64,96},{96,128},{128,160},{160,192},{192,224},{224... | collective-permute-start | bytes 1277960 | tf_op jit(solution)/shard_map/ppermute | solution.py:48
  18.5 27.8 %collective-permute-start.5 = (bf16[32,6656]{1,0:T(8,128)(2,1)}, bf16[32,6656]{1,0:T(8,128)(2,1)}, u32[]{:S(2)}, u32[]{:S(2)}) collective-permute-start(bf16[32,6656]{1,0:T(8,128)(2,1)} %collective-permute-done.4), channel_id=1, source_target_pairs={{0,224},{32,0},{64,32},{96,64},{128,96},{160,128},{192,160},{224,1... | collective-permute-start | bytes 1277960 | tf_op jit(solution)/shard_map/ppermute | solution.py:50
  27.4 21.3 %collective-permute-start.3 = (bf16[32,6656]{1,0:T(8,128)(2,1)}, bf16[32,6656]{1,0:T(8,128)(2,1)}, u32[]{:S(2)}, u32[]{:S(2)}) collective-permute-start(bf16[32,6656]{1,0:T(8,128)(2,1)} %collective-permute-done.2), channel_id=1, source_target_pairs={{0,32},{32,64},{64,96},{96,128},{128,160},{160,192},{192,224},{224... | collective-permute-start | bytes 1277960 | tf_op jit(solution)/shard_map/ppermute | solution.py:48
  34.9 49.1 %all-to-all-start.1 = ((f32[32,1,896]{2,1,0:T(1,128)}), f32[32,1,896]{2,1,0:T(1,128)S(1)}, u32[]{:S(2)}, u32[]{:S(2)}) async-start(f32[32,1,896]{2,1,0:T(1,128)} %broadcast_in_dim.2), calls=%async_computation.1 | async-start | bytes 229376 | tf_op jit(solution)/shard_map/all_to_all | solution.py:34
  46.2 25.9 %copy-start = (bf16[896,6656]{1,0:T(8,128)(2,1)S(1)}, bf16[896,6656]{1,0:T(8,128)(2,1)}, u32[]{:S(2)}) copy-start(bf16[896,6656]{1,0:T(8,128)(2,1)} %param.2) | copy-start | bytes 35782660
  46.3 13.7 %collective-permute-start.6 = (bf16[32,6656]{1,0:T(8,128)(2,1)}, bf16[32,6656]{1,0:T(8,128)(2,1)S(1)}, u32[]{:S(2)}, u32[]{:S(2)}) collective-permute-start(bf16[32,6656]{1,0:T(8,128)(2,1)} %collective-permute-done.5), channel_id=1, source_target_pairs={{0,224},{32,0},{64,32},{96,64},{128,96},{160,128},{192,160},{224,1... | collective-permute-start | bytes 1277960 | tf_op jit(solution)/shard_map/ppermute | solution.py:50
  84.0 36.2 %all-to-all-start = ((f32[32,8,897]{2,1,0:T(8,128)}), f32[32,8,897]{2,1,0:T(8,128)S(1)}, u32[]{:S(2)}, u32[]{:S(2)}) async-start(f32[32,8,897]{2,1,0:T(8,128)} %pad_maximum_fusion), calls=%async_computation | async-start | bytes 2097152 | tf_op jit(solution)/shard_map/all_to_all | solution.py:17
